TPU v7x, 32 devices: a whole 2x2x4 slice. The times are simulated.
32 devices in a mesh: pool: 4 (over y, core), ga: 8 (over z, x).
Axes of the slice: x: 2, y: 2, z: 4, core: 2. Of those that a mesh axis runs over, the one named last changes fastest.
Arguments:
- coefficients: bfloat16 [4, 256, 2, 256, 128], P('pool', 'ga'), may hold values from -6 to 6
- stick_count: int32 [4, 8], P('pool', 'ga'), may hold values from 28 to 32, as said below
- dest_device: int32 [4, 256], P('pool', 'ga'), may hold values from -1 to 7, as said below
- dest_slot: int32 [4, 256], P('pool', 'ga'), may hold values from -1 to 31, as said below
- source_stick: int32 [4, 256], P('pool', 'ga'), may hold values from -1 to 255, as said below
Outputs:
- margins: float32 [4, 2, 256, 256], P('pool', None, 'ga')
Inputs may be any that keep to these rules, and one draw needn't show every extreme that they name: Every k-point has a device whose 32 slots are all live; a device's live sticks are its first stick_count slots. `dest_device`: -1 exactly for sticks that land nowhere (among them all sticks that are not live); no device sends more than 8 of its sticks to one device, and some pair of devices reaches 8 for every k-point. `dest_slot`: -1 where dest_device is -1; the slots named are live slots of the layout of k-point q-1, no slot named twice. `source_stick`: the exact inverse of dest_device and dest_slot: a slot names a stick exactly when that stick names the slot, else -1.
All inputs are finite; a program needn't handle non-finite values.
Results may differ from a plain program's by a relative error of at most 0.0003.
Values may be sent and summed in bfloat16 or wider, within the bound.
No kernel may reach another device: no remote copies, remote signals or barrier semaphores. Data moves between devices by JAX's collectives and lax.ppermute only.
A program may use at most 64 MiB of HBM per device.

v0:
```python
import jax
import jax.numpy as jnp
from jax import lax
from jax.sharding import PartitionSpec as P


def passed_along(value, axis, steps):
    count = lax.axis_size(axis)
    pairs = [(source, (source + steps) % count) for source in range(count)]
    return lax.ppermute(value, axis, pairs)


def margin(bra_rows, ket_rows, slot_count, bands, plane_waves):
    bra_block = bra_rows.reshape(slot_count, 2, bands, plane_waves)
    ket_block = ket_rows.reshape(slot_count, 2, bands, plane_waves)
    swapped = jnp.stack([ket_block[:, 1], -ket_block[:, 0]], axis=1)
    real_part = jnp.einsum(
        "scmg,scng->mn", bra_block, ket_block, preferred_element_type=jnp.float32
    )
    imag_part = jnp.einsum("scmg,scng->mn", bra_block, swapped, preferred_element_type=jnp.float32)
    return jnp.stack([real_part, imag_part])


def owner_rows(partial_value, groups, bands, norm_scale):
    row_count = bands // groups
    totals = lax.psum(partial_value, "ga")
    owned = lax.dynamic_slice_in_dim(totals, lax.axis_index("ga") * row_count, row_count, 1)
    return owned * norm_scale


def local(coefficients, stick_count, dest_device, dest_slot, source_stick):
    groups = lax.axis_size("ga")
    slot_count = coefficients.shape[1]
    bands = coefficients.shape[3]
    plane_waves = coefficients.shape[4]
    pair_cap = max(2, (2 * slot_count + groups - 1) // groups)
    buffer_rows = groups * pair_cap
    norm_scale = (2 * groups * slot_count * plane_waves) ** (-0.5)
    coef_rows = coefficients.reshape(slot_count, -1)
    slot_list = jnp.arange(slot_count, dtype=jnp.int32)
    buffer_list = jnp.arange(buffer_rows, dtype=jnp.int32)
    live_mask = slot_list < stick_count[0, 0]
    bra_rows = jnp.where(live_mask[:, None], coef_rows, jnp.zeros_like(coef_rows))
    targets = dest_device[0]
    dest_order = dest_slot[0]
    matching = targets[:, None] == targets[None, :]
    earlier = dest_order[None, :] < dest_order[:, None]
    ranking = jnp.sum((matching & earlier).astype(jnp.int32), axis=1)
    position = jnp.where(targets >= 0, targets * pair_cap + ranking, -1)
    packer = (buffer_list[:, None] == position[None, :]).astype(jnp.bfloat16)
    outgoing = jnp.dot(packer, coef_rows, preferred_element_type=jnp.float32).astype(jnp.bfloat16)
    outgoing = outgoing.reshape(groups, pair_cap, -1)
    incoming = lax.all_to_all(outgoing, "ga", split_axis=0, concat_axis=0, tiled=True)
    anchor = source_stick[0]
    source_dev = jnp.where(anchor >= 0, anchor // slot_count, -1)
    matching_in = source_dev[:, None] == source_dev[None, :]
    earlier_in = slot_list[None, :] < slot_list[:, None]
    ranking_in = jnp.sum((matching_in & earlier_in).astype(jnp.int32), axis=1)
    position_in = jnp.where(anchor >= 0, source_dev * pair_cap + ranking_in, -1)
    placer = (position_in[:, None] == buffer_list[None, :]).astype(jnp.bfloat16)
    ket_rows = jnp.dot(
        placer, incoming.reshape(buffer_rows, -1), preferred_element_type=jnp.float32
    ).astype(jnp.bfloat16)
    bra_here = passed_along(bra_rows, "pool", 1)
    partial_value = margin(bra_here, ket_rows, slot_count, bands, plane_waves)
    finished = owner_rows(partial_value, groups, bands, norm_scale)
    result = passed_along(finished, "pool", -1)
    return result[None]


def solution(mesh):
    return jax.shard_map(
        local,
        mesh=mesh,
        in_specs=(
            P("pool", "ga", None, None, None),
            P("pool", "ga"),
            P("pool", "ga"),
            P("pool", "ga"),
            P("pool", "ga"),
        ),
        out_specs=P("pool", None, "ga", None),
        check_vma=False,
    )
```

profile of v0, /device:TPU:1, one launch (start us, length us, event | category | flops | bytes accessed | tf_op | source)
XLA Modules:
  0.0 305.1 jit_solution(17752583700953156419)
XLA Ops:
  6.5 5.6 %reshape.71 = bf16[32,65536]{1,0:T(8,128)(2,1)} reshape(bf16[1,32,2,256,128]{4,3,2,1,0:T(8,128)(2,1)} %param.5) | data formatting | bytes 8388608 | tf_op jit(solution)/shard_map/reshape | solution.py:39
  12.1 0.2 convert_reduce_fusion
  12.3 7.7 %fusion = bf16[8,8,65536]{2,1,0:T(8,128)(2,1)} fusion(bf16[32,65536]{1,0:T(8,128)(2,1)} %reshape.71, s32[32]{0:T(128)S(1)} %fusion.23), kind=kOutput, calls=%fused_computation.1 | convolution fusion | flops 272631808 | bytes 12583040 | tf_op jit(solution)/shard_map/dot_general | solution.py:51
  20.0 6.3 %all-to-all-start = ((bf16[8,8,65536]{2,1,0:T(8,128)(2,1)}), bf16[8,8,65536]{2,1,0:T(8,128)(2,1)}, u32[]{:S(2)}, u32[]{:S(2)}) async-start(bf16[8,8,65536]{2,1,0:T(8,128)(2,1)} %fusion), calls=%async_computation | async-start | bytes 16777216 | tf_op jit(solution)/shard_map/all_to_all | solution.py:53
  26.4 0.0 all-reduce.2.cloned.1.call-start
  27.1 2.5 broadcast_select_fusion
  29.6 2.1 collective-permute-start
  31.8 0.2 convert_reduce_fusion.1
  32.0 45.2 %collective-permute-done = bf16[32,65536]{1,0:T(8,128)(2,1)S(1)} collective-permute-done((bf16[32,65536]{1,0:T(8,128)(2,1)S(1)}, bf16[32,65536]{1,0:T(8,128)(2,1)S(1)}, u32[]{:S(2)}, u32[]{:S(2)}) %collective-permute-start) | collective-permute-done | bytes 4194336 | tf_op jit(solution)/shard_map/ppermute | solution.py:10
  77.2 2.9 copy.21
  80.1 128.7 %all-to-all-done = bf16[8,8,65536]{2,1,0:T(8,128)(2,1)} async-done(((bf16[8,8,65536]{2,1,0:T(8,128)(2,1)}), bf16[8,8,65536]{2,1,0:T(8,128)(2,1)}, u32[]{:S(2)}, u32[]{:S(2)}) %all-to-all-start) | async-done | bytes 8388640 | tf_op jit(solution)/shard_map/all_to_all | solution.py:53
  208.7 4.7 %fusion.9 = bf16[4,8,512,128]{3,1,2,0:T(8,128)(2,1)S(1)} fusion(bf16[8,8,65536]{2,1,0:T(8,128)(2,1)} %all-to-all-done, s32[32]{0:T(128)S(1)} %compare_select_fusion.8), kind=kOutput, calls=%fused_computation.12 | convolution fusion | flops 270534656 | bytes 12583040 | tf_op jit(solution)/shard_map/dot_general | solution.py:61
  213.4 1.0 copy.22
  214.4 0.8 fusion.27
  215.2 1.4 copy-done
  216.6 1.3 fusion.12
  217.9 1.3 fusion.15
  219.1 0.8 pad_maximum_fusion
  220.0 0.0 all-reduce.2.cloned.1.call-update
  220.0 71.4 %all-reduce.2.cloned.1.call-done = f32[2,256,256]{2,1,0:T(8,128)} async-done(((f32[2,256,256]{2,1,0:T(8,128)}), f32[2,256,256]{2,1,0:T(8,128)}) %all-reduce.2.cloned.1.call-update) | async-done | bytes 524304 | tf_op jit(solution)/shard_map/psum | solution.py:26
  291.4 0.8 dynamic-slice_multiply_fusion
  292.2 2.4 collective-permute-start.1
  294.6 3.0 collective-permute-done.1
  297.6 0.6 copy.38
  (12 shorter events, 0.1 us)
Async XLA Ops:
  6.5 5.6 %copy-start.2 = (s32[1,32]{1,0:T(1,128)S(1)}, s32[1,32]{1,0:T(1,128)}, u32[]{:S(2)}) copy-start(s32[1,32]{1,0:T(1,128)} %param.7) | copy-start | bytes 388
  6.5 5.6 %copy-start.1 = (s32[1,32]{1,0:T(1,128)S(1)}, s32[1,32]{1,0:T(1,128)}, u32[]{:S(2)}) copy-start(s32[1,32]{1,0:T(1,128)} %param.8) | copy-start | bytes 388
  20.0 188.7 %all-to-all-start = ((bf16[8,8,65536]{2,1,0:T(8,128)(2,1)}), bf16[8,8,65536]{2,1,0:T(8,128)(2,1)}, u32[]{:S(2)}, u32[]{:S(2)}) async-start(bf16[8,8,65536]{2,1,0:T(8,128)(2,1)} %fusion), calls=%async_computation | async-start | bytes 16777216 | tf_op jit(solution)/shard_map/all_to_all | solution.py:53
  26.4 265.0 %all-reduce.2.cloned.1.call-start = ((), (), s32[]{:S(2)}) async-start(), calls=%async_computation.1 | async-start | bytes 1048576 | tf_op jit(solution)/shard_map/psum | solution.py:26
  27.1 4.7 %copy-start.3 = (s32[1,32]{1,0:T(1,128)S(1)}, s32[1,32]{1,0:T(1,128)}, u32[]{:S(2)}) copy-start(s32[1,32]{1,0:T(1,128)} %param.9) | copy-start | bytes 388
  29.6 47.6 %collective-permute-start = (bf16[32,65536]{1,0:T(8,128)(2,1)S(1)}, bf16[32,65536]{1,0:T(8,128)(2,1)S(1)}, u32[]{:S(2)}, u32[]{:S(2)}) collective-permute-start(bf16[32,65536]{1,0:T(8,128)(2,1)S(1)} %broadcast_select_fusion), channel_id=1, source_target_pairs={{0,8},{8,16},{16,24},{24,0},{1,9},{9,17},{17,25},{25,1},{2,10},{10... | collective-permute-start | bytes 12582920 | tf_op jit(solution)/shard_map/ppermute | solution.py:10
  214.4 2.2 copy-start
  292.2 5.4 %collective-permute-start.1 = (f32[2,32,256]{2,1,0:T(8,128)S(1)}, f32[2,32,256]{2,1,0:T(8,128)S(1)}, u32[]{:S(2)}, u32[]{:S(2)}) collective-permute-start(f32[2,32,256]{2,1,0:T(8,128)S(1)} %dynamic-slice_multiply_fusion), channel_id=1, source_target_pairs={{0,24},{8,0},{16,8},{24,16},{1,25},{9,1},{17,9},{25,17},{2,26},{10... | collective-permute-start | bytes 196616 | tf_op jit(solution)/shard_map/ppermute | solution.py:10
Sparse Core Ops, SparseCore 0:
  220.1 71.2 all-reduce.1
where the time goes:
time: 306 us; the launch traced here: 305 us
  waiting for transfers between devices  248 us (81%)
  matrix products  15 us (5%)
  between operations  14.1 us (5%)
  local copies, waits for them, and re-layouts  11.5 us (4%)
  starting transfers between devices  10.9 us (4%)
  other arithmetic  5.37 us (2%)
    all_to_all x1, waiting for transfers between devices, local(): lax.all_to_all(outgoing, 'ga', split_axis=0, concat_axis=0, tiled=True)  129 us
    psum x1, waiting for transfers between devices, owner_rows(): totals = lax.psum(partial_value, 'ga')  71.4 us
    ppermute x2, waiting for transfers between devices, passed_along(): return lax.ppermute(value, axis, pairs)  48.2 us
    dot_general x1, matrix products, local(): jnp.dot(packer, coef_rows, preferred_element_type=jnp.float32)  7.73 us
    all_to_all x1, starting transfers between devices, local(): lax.all_to_all(outgoing, 'ga', split_axis=0, concat_axis=0, tiled=True)  6.34 us
  transfers between devices with their start and end apart: 4, of which 4 were waited for; matrix products, arithmetic and copies ran while one was open for 2% of the time, Pallas kernels for 0%

commit v1 on v0

--- a/solution.py
+++ b/solution.py
@@ -2,6 +2,14 @@
 import jax.numpy as jnp
 from jax import lax
 from jax.sharding import PartitionSpec as P
+
+
+def added_up(value, mesh_axis):
+    count, summed = (lax.axis_size(mesh_axis), value)
+    for stride in [1 << k for k in range(count.bit_length() - 1)]:
+        pairs = [(i, i ^ stride) for i in range(count)]
+        summed = summed + lax.ppermute(summed, mesh_axis, pairs)
+    return summed
 
 
 def passed_along(value, axis, steps):
@@ -23,7 +31,7 @@
 
 def owner_rows(partial_value, groups, bands, norm_scale):
     row_count = bands // groups
-    totals = lax.psum(partial_value, "ga")
+    totals = added_up(partial_value, "ga")
     owned = lax.dynamic_slice_in_dim(totals, lax.axis_index("ga") * row_count, row_count, 1)
     return owned * norm_scale
 

time: 306 us -> 269 us (0.88)
  waiting for transfers between devices: 248 us -> 220 us
  between operations: 14.1 us -> 0.76 us
  starting transfers between devices: 10.9 us -> 17.3 us
    psum x1 -> x0, waiting for transfers between devices: 71.4 us -> none  [owner_rows(): totals = lax.psum(partial_value, 'ga')]
    ppermute x0 -> x3, waiting for transfers between devices: none -> 43 us  [added_up(): summed = summed + lax.ppermute(summed, mesh_axis, pairs)]
    ppermute x0 -> x3, starting transfers between devices: none -> 7.41 us  [added_up(): summed = summed + lax.ppermute(summed, mesh_axis, pairs)]
  transfers between devices with their start and end apart: 4 -> 6, of which waited for: 4 -> 6; matrix products, arithmetic and copies ran while one was open for 2% -> 2% of each run, Pallas kernels for 0% -> 0%
where the time goes in v1:
time: 269 us; the launch traced here: 268 us
  waiting for transfers between devices  220 us (82%)
  starting transfers between devices  17.3 us (6%)
  matrix products  15 us (6%)
  local copies, waits for them, and re-layouts  11.4 us (4%)
  other arithmetic  3.95 us (1%)
    all_to_all x1, waiting for transfers between devices, local(): lax.all_to_all(outgoing, 'ga', split_axis=0, concat_axis=0, tiled=True)  129 us
    ppermute x2, waiting for transfers between devices, passed_along(): return lax.ppermute(value, axis, pairs)  48.3 us
    ppermute x3, waiting for transfers between devices, added_up(): summed = summed + lax.ppermute(summed, mesh_axis, pairs)  43 us
    dot_general x1, matrix products, local(): jnp.dot(packer, coef_rows, preferred_element_type=jnp.float32)  7.72 us
    ppermute x3, starting transfers between devices, added_up(): summed = summed + lax.ppermute(summed, mesh_axis, pairs)  7.41 us
    all_to_all x1, starting transfers between devices, local(): lax.all_to_all(outgoing, 'ga', split_axis=0, concat_axis=0, tiled=True)  6.34 us
    unnamed x11, local copies, waits for them, and re-layouts  5.86 us
    reshape x1, local copies, waits for them, and re-layouts, local(): coef_rows = coefficients.reshape(slot_count, -1)  5.57 us
  transfers between devices with their start and end apart: 6, of which 6 were waited for; matrix products, arithmetic and copies ran while one was open for 2% of the time, Pallas kernels for 0%

profile of v1, /device:TPU:1, one launch (start us, length us, event | category | flops | bytes accessed | tf_op | source)
XLA Modules:
  0.0 268.4 jit_solution(7769267728742006105)
XLA Ops:
  0.0 5.6 %reshape.71 = bf16[32,65536]{1,0:T(8,128)(2,1)} reshape(bf16[1,32,2,256,128]{4,3,2,1,0:T(8,128)(2,1)} %param.5) | data formatting | bytes 8388608 | tf_op jit(solution)/shard_map/reshape | solution.py:47
  5.8 7.7 %fusion = bf16[8,8,65536]{2,1,0:T(8,128)(2,1)} fusion(bf16[32,65536]{1,0:T(8,128)(2,1)} %reshape.71, s32[32]{0:T(128)S(1)} %get-tuple-element.7), kind=kOutput, calls=%fused_computation.1 | convolution fusion | flops 272631808 | bytes 12583040 | tf_op jit(solution)/shard_map/dot_general | solution.py:59
  13.5 6.3 %all-to-all-start = ((bf16[8,8,65536]{2,1,0:T(8,128)(2,1)}), bf16[8,8,65536]{2,1,0:T(8,128)(2,1)}, u32[]{:S(2)}, u32[]{:S(2)}) async-start(bf16[8,8,65536]{2,1,0:T(8,128)(2,1)} %fusion), calls=%async_computation | async-start | bytes 16777216 | tf_op jit(solution)/shard_map/all_to_all | solution.py:61
  20.5 2.5 broadcast_select_fusion
  23.1 2.1 collective-permute-start
  25.2 0.2 convert_reduce_fusion.1
  25.4 45.2 %collective-permute-done = bf16[32,65536]{1,0:T(8,128)(2,1)S(1)} collective-permute-done((bf16[32,65536]{1,0:T(8,128)(2,1)S(1)}, bf16[32,65536]{1,0:T(8,128)(2,1)S(1)}, u32[]{:S(2)}, u32[]{:S(2)}) %collective-permute-start) | collective-permute-done | bytes 4194336 | tf_op jit(solution)/shard_map/ppermute | solution.py:18
  70.6 2.9 %copy.21 = bf16[4,8,512,128]{3,2,1,0:T(8,128)(2,1)} copy(bf16[4,8,512,128]{3,1,2,0:T(8,128)(2,1)S(1)} %bitcast.57) | data formatting | bytes 8388608
  73.5 128.7 %all-to-all-done = bf16[8,8,65536]{2,1,0:T(8,128)(2,1)} async-done(((bf16[8,8,65536]{2,1,0:T(8,128)(2,1)}), bf16[8,8,65536]{2,1,0:T(8,128)(2,1)}, u32[]{:S(2)}, u32[]{:S(2)}) %all-to-all-start) | async-done | bytes 8388640 | tf_op jit(solution)/shard_map/all_to_all | solution.py:61
  202.2 4.7 %fusion.9 = bf16[4,8,512,128]{3,1,2,0:T(8,128)(2,1)S(1)} fusion(bf16[8,8,65536]{2,1,0:T(8,128)(2,1)} %all-to-all-done, s32[32]{0:T(128)S(1)} %compare_select_fusion.8), kind=kOutput, calls=%fused_computation.12 | convolution fusion | flops 270534656 | bytes 12583040 | tf_op jit(solution)/shard_map/dot_general | solution.py:69
  206.9 1.0 copy.22
  207.9 0.8 fusion.29
  208.7 1.4 copy-done
  210.1 1.3 fusion.12
  211.4 1.3 fusion.15
  212.7 1.6 collective-permute-start.1
  214.3 10.3 %collective-permute-done.1 = f32[2,256,256]{2,1,0:T(8,128)S(1)} collective-permute-done((f32[2,256,256]{2,1,0:T(8,128)S(1)}, f32[2,256,256]{2,1,0:T(8,128)S(1)}, u32[]{:S(2)}, u32[]{:S(2)}) %collective-permute-start.1) | collective-permute-done | bytes 524320 | tf_op jit(solution)/shard_map/ppermute | solution.py:11
  224.7 1.6 collective-permute-start.2
  226.3 9.9 %collective-permute-done.2 = f32[2,256,256]{2,1,0:T(8,128)S(1)} collective-permute-done((f32[2,256,256]{2,1,0:T(8,128)S(1)}, f32[2,256,256]{2,1,0:T(8,128)S(1)}, u32[]{:S(2)}, u32[]{:S(2)}) %collective-permute-start.2) | collective-permute-done | bytes 524320 | tf_op jit(solution)/shard_map/ppermute | solution.py:11
  236.4 4.2 %collective-permute-start.3 = (f32[2,256,256]{2,1,0:T(8,128)S(1)}, f32[2,256,256]{2,1,0:T(8,128)S(1)}, u32[]{:S(2)}, u32[]{:S(2)}) collective-permute-start(f32[2,256,256]{2,1,0:T(8,128)S(1)} %fusion.31), channel_id=1, source_target_pairs={{0,4},{1,5},{2,6},{3,7},{4,0},{5,1},{6,2},{7,3},{8,12},{9,13},{10,... | collective-permute-start | bytes 1572872 | tf_op jit(solution)/shard_map/ppermute | solution.py:11
  240.6 22.7 %collective-permute-done.3 = f32[2,256,256]{2,1,0:T(8,128)S(1)} collective-permute-done((f32[2,256,256]{2,1,0:T(8,128)S(1)}, f32[2,256,256]{2,1,0:T(8,128)S(1)}, u32[]{:S(2)}, u32[]{:S(2)}) %collective-permute-start.3) | collective-permute-done | bytes 524320 | tf_op jit(solution)/shard_map/ppermute | solution.py:11
  263.3 1.4 collective-permute-start.4
  264.8 3.0 %collective-permute-done.4 = f32[2,32,256]{2,1,0:T(8,128)S(1)} collective-permute-done((f32[2,32,256]{2,1,0:T(8,128)S(1)}, f32[2,32,256]{2,1,0:T(8,128)S(1)}, u32[]{:S(2)}, u32[]{:S(2)}) %collective-permute-start.4) | collective-permute-done | bytes 65568 | tf_op jit(solution)/shard_map/ppermute | solution.py:18
  267.8 0.6 copy.37
  (16 shorter events, 0.5 us)
Async XLA Ops:
  0.0 5.6 %copy-start.1 = (s32[1,32]{1,0:T(1,128)S(1)}, s32[1,32]{1,0:T(1,128)}, u32[]{:S(2)}) copy-start(s32[1,32]{1,0:T(1,128)} %param.7) | copy-start | bytes 388
  0.0 5.6 %copy-start.2 = (s32[1,32]{1,0:T(1,128)S(1)}, s32[1,32]{1,0:T(1,128)}, u32[]{:S(2)}) copy-start(s32[1,32]{1,0:T(1,128)} %param.8) | copy-start | bytes 388
  0.0 5.8 %copy-start.3 = (s32[1,32]{1,0:T(1,128)S(1)}, s32[1,32]{1,0:T(1,128)}, u32[]{:S(2)}) copy-start(s32[1,32]{1,0:T(1,128)} %param.9) | copy-start | bytes 388
  13.5 188.7 %all-to-all-start = ((bf16[8,8,65536]{2,1,0:T(8,128)(2,1)}), bf16[8,8,65536]{2,1,0:T(8,128)(2,1)}, u32[]{:S(2)}, u32[]{:S(2)}) async-start(bf16[8,8,65536]{2,1,0:T(8,128)(2,1)} %fusion), calls=%async_computation | async-start | bytes 16777216 | tf_op jit(solution)/shard_map/all_to_all | solution.py:61
  23.1 47.6 %collective-permute-start = (bf16[32,65536]{1,0:T(8,128)(2,1)S(1)}, bf16[32,65536]{1,0:T(8,128)(2,1)S(1)}, u32[]{:S(2)}, u32[]{:S(2)}) collective-permute-start(bf16[32,65536]{1,0:T(8,128)(2,1)S(1)} %broadcast_select_fusion), channel_id=1, source_target_pairs={{0,8},{8,16},{16,24},{24,0},{1,9},{9,17},{17,25},{25,1},{2,10},{10... | collective-permute-start | bytes 12582920 | tf_op jit(solution)/shard_map/ppermute | solution.py:18
  207.9 2.2 copy-start
  212.7 12.0 %collective-permute-start.1 = (f32[2,256,256]{2,1,0:T(8,128)S(1)}, f32[2,256,256]{2,1,0:T(8,128)S(1)}, u32[]{:S(2)}, u32[]{:S(2)}) collective-permute-start(f32[2,256,256]{2,1,0:T(8,128)S(1)} %pad_maximum_fusion), channel_id=1, source_target_pairs={{0,1},{1,0},{2,3},{3,2},{4,5},{5,4},{6,7},{7,6},{8,9},{9,8},{10,11... | collective-permute-start | bytes 1572872 | tf_op jit(solution)/shard_map/ppermute | solution.py:11
  224.7 11.6 %collective-permute-start.2 = (f32[2,256,256]{2,1,0:T(8,128)S(1)}, f32[2,256,256]{2,1,0:T(8,128)S(1)}, u32[]{:S(2)}, u32[]{:S(2)}) collective-permute-start(f32[2,256,256]{2,1,0:T(8,128)S(1)} %fusion.27), channel_id=1, source_target_pairs={{0,2},{1,3},{2,0},{3,1},{4,6},{5,7},{6,4},{7,5},{8,10},{9,11},{10,... | collective-permute-start | bytes 1572872 | tf_op jit(solution)/shard_map/ppermute | solution.py:11
  236.4 26.9 %collective-permute-start.3 = (f32[2,256,256]{2,1,0:T(8,128)S(1)}, f32[2,256,256]{2,1,0:T(8,128)S(1)}, u32[]{:S(2)}, u32[]{:S(2)}) collective-permute-start(f32[2,256,256]{2,1,0:T(8,128)S(1)} %fusion.31), channel_id=1, source_target_pairs={{0,4},{1,5},{2,6},{3,7},{4,0},{5,1},{6,2},{7,3},{8,12},{9,13},{10,... | collective-permute-start | bytes 1572872 | tf_op jit(solution)/shard_map/ppermute | solution.py:11
  263.3 4.5 %collective-permute-start.4 = (f32[2,32,256]{2,1,0:T(8,128)S(1)}, f32[2,32,256]{2,1,0:T(8,128)S(1)}, u32[]{:S(2)}, u32[]{:S(2)}) collective-permute-start(f32[2,32,256]{2,1,0:T(8,128)S(1)} %fusion.20), channel_id=1, source_target_pairs={{0,24},{8,0},{16,8},{24,16},{1,25},{9,1},{17,9},{25,17},{2,26},{10... | collective-permute-start | bytes 196616 | tf_op jit(solution)/shard_map/ppermute | solution.py:18
